TPU v7x, 256 devices: a whole 4x4x8 slice. The times are simulated.
256 devices in a mesh: rows: 32 (over y, x, core), rhs: 8 (over z).
Axes of the slice: x: 4, y: 4, z: 8, core: 2. Of those that a mesh axis runs over, the one named last changes fastest.
Arguments:
- sources: bfloat16 [131072, 4096], P('rows', 'rhs'), may hold values from -6 to 6
- near_blocks: bfloat16 [512, 3, 256, 256], P('rows'), may hold values from -0.21875 to 0.21875
- near_list: int32 [512, 3], P('rows'), may hold values from 0 to 511, as said below
- source_basis: bfloat16 [512, 256, 32], P('rows'), may hold values from -0.375 to 0.375
- target_basis: bfloat16 [512, 256, 32], P('rows'), may hold values from -0.375 to 0.375
- transfer_fine: bfloat16 [896, 32, 32], P('rows'), may hold values from -0.875 to 0.875
- transfer_coarse: bfloat16 [128, 32, 32], P('rhs'), may hold values from -0.875 to 0.875
- couple_fine: bfloat16 [896, 3, 32, 32], P('rows'), may hold values from -0.625 to 0.625
- couple_coarse: bfloat16 [128, 3, 32, 32], P('rhs'), may hold values from -0.625 to 0.625
- far_fine: int32 [896, 3], P('rows'), may hold values from 0 to 511, as said below
- far_coarse: int32 [128, 3], replicated, may hold values from -1 to 63, as said below
Outputs:
- potentials: bfloat16 [131072, 4096], P('rows', 'rhs')
Inputs may be any that keep to these rules, and one draw needn't show every extreme that they name: `near_list`: row t lists the leaf clusters t - 1, t and t + 1 modulo 512 in some order. `far_fine`: row d * 28 + o + i belongs to cluster d * m + i of the level with n = m * 32 clusters, where (o, m) is (0, 16), (16, 8) or (24, 4). It lists, in some order, the three clusters of that level that are children of the cyclic neighbours of the cluster's parent and not cyclic neighbours of the cluster: for cluster j with parent p = j // 2, the clusters 2p - 2, 2p + 2, 2p + 3 if j is even and 2p - 2, 2p - 1, 2p + 3 if j is odd, modulo n. `far_coarse`: row n + j for n = 8, 16, ..., 64 lists, in some order, the three far clusters of cluster j of the level with n clusters by the rule of far_fine. Row 4 + j holds (j + 2) modulo 4 in slot 0 and -1 in slots 1 and 2. Rows 0 to 3 hold -1.
All inputs are finite; a program needn't handle non-finite values.
Results may differ from a plain program's by a relative error of at most 0.012.
Values may be sent and summed in bfloat16 or wider, within the bound.
A program may use at most 128 MiB of HBM per device.

v0:
```python
import jax
import jax.numpy as jnp
from jax import lax
from jax.sharding import PartitionSpec as P


def padded_2(cells, sides, width):
    for axis, dim in sides:
        count = lax.axis_size(axis)
        head = lax.slice_in_dim(cells, 0, width, axis=dim)
        tail = lax.slice_in_dim(cells, cells.shape[dim] - width, cells.shape[dim], axis=dim)
        cells = jnp.concatenate(
            [
                lax.ppermute(tail, axis, [(i, (i + 1) % count) for i in range(count)]),
                cells,
                lax.ppermute(head, axis, [((i + 1) % count, i) for i in range(count)]),
            ],
            axis=dim,
        )
    return cells


def from_everyone(shard, axis):
    copies = jnp.broadcast_to(shard, (lax.axis_size(axis), *shard.shape))
    return lax.all_to_all(copies, axis, split_axis=0, concat_axis=0, tiled=True)


def joined_along(pieces, dim):
    pieces = jnp.moveaxis(pieces, 0, dim)
    dims = pieces.shape
    return pieces.reshape(*dims[:dim], dims[dim] * dims[dim + 1], *dims[dim + 2 :])


def gather_directly(shard, axis, dim):
    pieces = from_everyone(shard, axis)
    return joined_along(pieces, dim)


def sent_together(arrays, axis, dim, along):
    columns = [a.reshape(*a.shape[:along], -1) for a in arrays]
    both = jnp.concatenate(columns, axis=along)
    whole, at, finished = (gather_directly(both, axis, dim), 0, [])
    for a, column in zip(arrays, columns):
        slab = whole[..., at : at + column.shape[along]]
        finished.append(slab.reshape(*slab.shape[:along], *a.shape[along:]))
        at += column.shape[along]
    return tuple(finished)


def couple_masked(moments, blocks, partners):
    valid = partners >= 0
    picked = moments[jnp.maximum(partners, 0)]
    picked = jnp.where(valid[:, :, None, None], picked, jnp.zeros_like(picked))
    return jnp.einsum("nsab,nsbr->nar", blocks, picked, preferred_element_type=jnp.float32)


def routed_blocks(blocks, offset, wanted):
    chosen = jnp.zeros_like(blocks[:, 0])
    for slot in range(3):
        match = (offset[:, slot] == wanted)[:, None, None]
        chosen = jnp.where(match, blocks[:, slot], chosen)
    return chosen


def couple_window(moments, blocks, partners, position, row_count):
    clusters = moments.shape[0]
    level_size = clusters * row_count
    window = padded_2(moments, (("rows", 0),), 3)
    targets = position * clusters + jnp.arange(clusters, dtype=jnp.int32)
    offset = (partners - targets[:, None] + level_size // 2) % level_size - level_size // 2
    coupled = jnp.zeros((clusters, moments.shape[1], moments.shape[2]), jnp.float32)
    for wanted in (-3, -2, 2, 3):
        chosen = routed_blocks(blocks, offset, wanted)
        shifted = window[3 + wanted : 3 + wanted + clusters]
        coupled = coupled + jnp.einsum(
            "nab,nbr->nar", chosen, shifted, preferred_element_type=jnp.float32
        )
    return coupled


def lift(moments, transfer):
    clusters, rank, width = moments.shape
    product = jnp.einsum("nab,nar->nbr", transfer, moments, preferred_element_type=jnp.float32)
    return product.reshape(clusters // 2, 2, rank, width).sum(axis=1).astype(jnp.bfloat16)


def lower(parent, transfer, coupled):
    spread = jnp.repeat(parent, 2, axis=0)
    carried = jnp.einsum("nab,nbr->nar", transfer, spread, preferred_element_type=jnp.float32)
    return (coupled + carried).astype(jnp.bfloat16)


def coarse_pass(moments, transfer_all, couple_all, far_all):
    clusters = moments.shape[0]
    depth = clusters.bit_length() - 3
    upward = [moments]
    for step in range(depth):
        moments = lift(moments, transfer_all[clusters : 2 * clusters])
        clusters = clusters // 2
        upward.append(moments)
    downward = moments
    for step in range(depth + 1):
        coupled = couple_masked(
            upward[depth - step],
            couple_all[clusters : 2 * clusters],
            far_all[clusters : 2 * clusters],
        )
        if step == 0:
            downward = coupled.astype(jnp.bfloat16)
        else:
            downward = lower(downward, transfer_all[clusters : 2 * clusters], coupled)
        clusters = clusters * 2
    return downward


def body(
    sources,
    near_blocks,
    near_list,
    source_basis,
    target_basis,
    transfer_fine,
    transfer_coarse,
    couple_fine,
    couple_coarse,
    far_fine,
    far_coarse,
):
    count = near_blocks.shape[0]
    leaf = near_blocks.shape[2]
    width = sources.shape[1]
    row_count = lax.axis_size("rows")
    position = lax.axis_index("rows")
    all_leaves = count * row_count
    padded = padded_2(sources, (("rows", 0),), leaf)
    neighbours = padded.reshape(count + 2, leaf, width)
    targets = position * count + jnp.arange(count, dtype=jnp.int32)
    offset = (near_list - targets[:, None] + all_leaves // 2) % all_leaves - all_leaves // 2
    near_part = jnp.zeros((count, leaf, width), jnp.float32)
    for wanted in (-1, 0, 1):
        chosen = routed_blocks(near_blocks, offset, wanted)
        shifted = neighbours[1 + wanted : 1 + wanted + count]
        near_part = near_part + jnp.einsum(
            "npq,nqr->npr", chosen, shifted, preferred_element_type=jnp.float32
        )
    shaped = sources.reshape(count, leaf, width)
    moments = jnp.einsum(
        "npk,npr->nkr", source_basis, shaped, preferred_element_type=jnp.float32
    ).astype(jnp.bfloat16)
    level_counts = [count, count // 2, count // 4]
    firsts = [0, count, count + count // 2]
    upward = [moments]
    for level in range(3):
        moments = lift(moments, transfer_fine[firsts[level] : firsts[level] + level_counts[level]])
        upward.append(moments)
    tables = sent_together((transfer_coarse, couple_coarse), "rhs", 0, 1)
    columns = lax.all_to_all(moments, "rows", split_axis=2, concat_axis=0, tiled=True)
    result = coarse_pass(columns, tables[0], tables[1], far_coarse)
    parents = lax.all_to_all(result, "rows", split_axis=0, concat_axis=2, tiled=True)
    downward = parents
    for level in (2, 1, 0):
        first = firsts[level]
        last = first + level_counts[level]
        coupled = couple_window(
            upward[level], couple_fine[first:last], far_fine[first:last], position, row_count
        )
        downward = lower(downward, transfer_fine[first:last], coupled)
    far_part = jnp.einsum(
        "npk,nkr->npr", target_basis, downward, preferred_element_type=jnp.float32
    )
    return (far_part + near_part).astype(jnp.bfloat16).reshape(count * leaf, width)


def solution(mesh):
    in_specs = (
        P("rows", "rhs"),
        P("rows", None, None, None),
        P("rows", None),
        P("rows", None, None),
        P("rows", None, None),
        P("rows", None, None),
        P("rhs", None, None),
        P("rows", None, None, None),
        P("rhs", None, None, None),
        P("rows", None),
        P(),
    )
    out_specs = P("rows", "rhs")
    return jax.shard_map(body, mesh=mesh, in_specs=in_specs, out_specs=out_specs, check_vma=False)
```

profile of v0, /device:TPU:1, one launch (start us, length us, event | category | flops | bytes accessed | tf_op | source)
XLA Modules:
  0.0 168.6 jit_solution(6814324130455730087)
XLA Ops:
  0.1 3.2 %convolution_convert_fusion = bf16[16,32,512]{2,1,0:T(8,128)(2,1)S(1)} fusion(bf16[16,256,32]{1,2,0:T(8,128)(2,1)} %param.14, bf16[16,256,512]{2,1,0:T(8,128)(2,1)} %bitcast.431), kind=kOutput, calls=%fused_computation.51 | convolution fusion | flops 134479872 | bytes 4980736 | tf_op jit(solution)/shard_map/npk,npr->nkr/dot_general | solution.py:147
  3.9 2.6 %collective-permute-start = (bf16[3,32,512]{2,1,0:T(8,128)(2,1)}, bf16[3,32,512]{2,1,0:T(8,128)(2,1)S(1)}, u32[]{:S(2)}, u32[]{:S(2)}) collective-permute-start(bf16[3,32,512]{2,1,0:T(8,128)(2,1)} %get-tuple-element.9), channel_id=1, source_target_pairs={{0,8},{8,16},{16,24},{24,32},{32,40},{40,48},{48,56},{56,64},{64,7... | collective-permute-start | bytes 294920 | tf_op jit(solution)/shard_map/ppermute | solution.py:14
  9.0 8.5 %all-to-all-start.1 = ((bf16[32,2,512]{2,1,0:T(2,128)(2,1)}), bf16[32,2,512]{2,1,0:T(2,128)(2,1)S(1)}, u32[]{:S(2)}, u32[]{:S(2)}) async-start(bf16[32,2,512]{2,1,0:T(2,128)(2,1)} %reshape.478), calls=%async_computation.1 | async-start | bytes 131072 | tf_op jit(solution)/shard_map/all_to_all | solution.py:157
  18.2 1.6 collective-permute-start.4
  20.5 3.8 %collective-permute-start.3 = (bf16[3,32,512]{2,1,0:T(8,128)(2,1)S(1)}, bf16[3,32,512]{2,1,0:T(8,128)(2,1)S(1)}, u32[]{:S(2)}, u32[]{:S(2)}) collective-permute-start(bf16[3,32,512]{2,1,0:T(8,128)(2,1)S(1)} %get-tuple-element.12), channel_id=1, source_target_pairs={{8,0},{16,8},{24,16},{32,24},{40,32},{48,40},{56,48},{64,56},{72,6... | collective-permute-start | bytes 294920 | tf_op jit(solution)/shard_map/ppermute | solution.py:16
  25.0 1.8 %fusion.297 = (bf16[256,512]{1,0:T(8,128)(2,1)}, bf16[256,512]{1,0:T(8,128)(2,1)S(1)}) fusion(bf16[4096,512]{1,0:T(8,128)(2,1)} %param.11), kind=kLoop, calls=%fused_computation.404 | loop fusion | bytes 1048576 | tf_op jit(solution)/shard_map/slice | solution.py:10
  36.8 8.7 %fusion.7 = f32[16,256,512]{2,1,0:T(8,128)} fusion(bf16[16,256,512]{2,1,0:T(8,128)(2,1)} %bitcast.432, pred[16]{0:T(512)(128)(4,1)S(1)} %get-tuple-element.19, pred[16]{0:T(512)(128)(4,1)S(1)} %get-tuple-element.17, pred[16]{0:T(512)(128)(4,1)S(1)} %get-tuple-element.16, bf16[16,3,256,256]{3,2,1,0:T(8,128)(2,1)} %param.12), kind=kOutput, calls=%fused_computation.17 | convolution fusion | flops 1076887552 | bytes 18874416 | tf_op jit(solution)/shard_map/npq,nqr->npr/dot_general | solution.py:143
  45.5 1.1 broadcast_in_dim.421
  46.6 6.8 %all-to-all-start = ((bf16[8,16,4096]{2,1,0:T(8,128)(2,1)}), bf16[8,16,4096]{2,1,0:T(8,128)(2,1)}, u32[]{:S(2)}, u32[]{:S(2)}) async-start(bf16[8,16,4096]{2,1,0:T(8,128)(2,1)} %broadcast_in_dim.421), calls=%async_computation | async-start | bytes 2097152 | tf_op jit(solution)/shard_map/all_to_all | solution.py:25
  53.6 1.6 gather_fusion
  55.4 2.0 %fusion.80 = f32[8,32,512]{2,1,0:T(8,128)} fusion(bf16[3,32,512]{2,1,0:T(8,128)(2,1)S(1)} %collective-permute-done.3, bf16[8,32,512]{2,1,0:T(8,128)(2,1)S(1)} %bitcast_reduce_fusion, pred[8]{0:T(512)(128)(4,1)S(1)} %get-tuple-element.45, pred[8]{0:T(512)(128)(4,1)S(1)} %get-tuple-element.42, pred[8]{0:T(512)(128)(4,1)S(1)} %get-tuple-element.39, ...), kind=kOutput, calls=%fused_computation.111 | convolution fusion | flops 8544256 | bytes 1081368 | tf_op jit(solution)/shard_map/nab,nbr->nar/dot_general | solution.py:75
  58.0 1.6 fusion.68
  59.7 2.0 %fusion.76 = f32[8,32,512]{2,1,0:T(8,128)} fusion(bf16[8,32,512]{2,1,0:T(8,128)(2,1)S(1)} %bitcast_reduce_fusion, bf16[3,32,512]{2,1,0:T(8,128)(2,1)S(1)} %collective-permute-done.3, pred[8]{0:T(512)(128)(4,1)S(1)} %copy-done.42, pred[8]{0:T(512)(128)(4,1)S(1)} %copy-done.41, pred[8]{0:T(512)(128)(4,1)S(1)} %copy-done.40, bf16[28,3,32,32]{3,2,1,0:T(8,128)(2,1)} %param.18), kind=kOutput, calls=%fused_computation.108 | convolution fusion | flops 8544256 | bytes 1081368 | tf_op jit(solution)/shard_map/nab,nbr->nar/dot_general | solution.py:75
  61.7 1.1 collective-permute-start.6
  62.8 2.0 %fusion.82 = f32[8,32,512]{2,1,0:T(8,128)} fusion(bf16[8,32,512]{2,1,0:T(8,128)(2,1)S(1)} %bitcast_reduce_fusion, bf16[3,32,512]{2,1,0:T(8,128)(2,1)S(1)} %collective-permute-done.2, pred[8]{0:T(512)(128)(4,1)S(1)} %get-tuple-element.43, pred[8]{0:T(512)(128)(4,1)S(1)} %get-tuple-element.40, pred[8]{0:T(512)(128)(4,1)S(1)} %get-tuple-element.37, ...), kind=kOutput, calls=%fused_computation.114 | convolution fusion | flops 8544256 | bytes 1081368 | tf_op jit(solution)/shard_map/nab,nbr->nar/dot_general | solution.py:75
  64.8 1.7 %fusion.92 = f32[4,32,512]{2,1,0:T(8,128)} fusion(bf16[3,32,512]{2,1,0:T(8,128)(2,1)S(1)} %collective-permute-done.5, bf16[4,32,512]{2,1,0:T(8,128)(2,1)S(1)} %bitcast_reduce_fusion.1, pred[4]{0:T(512)(128)(4,1)S(1)} %get-tuple-element.57, pred[4]{0:T(512)(128)(4,1)S(1)} %get-tuple-element.54, pred[4]{0:T(512)(128)(4,1)S(1)} %get-tuple-element.51, ...), kind=kOutput, calls=%fused_computation.129 | convolution fusion | flops 4272128 | bytes 589836 | tf_op jit(solution)/shard_map/nab,nbr->nar/dot_general | solution.py:75
  66.5 2.4 %fusion.63 = f32[16,32,512]{2,1,0:T(8,128)} fusion(bf16[16,32,512]{2,1,0:T(8,128)(2,1)S(1)} %convolution_convert_fusion, bf16[3,32,512]{2,1,0:T(8,128)(2,1)} %copy-done.15, pred[16]{0:T(512)(128)(4,1)S(1)} %copy-done.45, pred[16]{0:T(512)(128)(4,1)S(1)} %copy-done.44, pred[16]{0:T(512)(128)(4,1)S(1)} %copy-done.43, bf16[28,3,32,32]{3,2,1,0:T(8,128)(2,1)} %param.18), kind=kOutput, calls=%fused_computation.90 | convolution fusion | flops 17088512 | bytes 2064432 | tf_op jit(solution)/shard_map/nab,nbr->nar/dot_general | solution.py:75
  68.9 1.7 %fusion.88 = f32[4,32,512]{2,1,0:T(8,128)} fusion(bf16[4,32,512]{2,1,0:T(8,128)(2,1)S(1)} %bitcast_reduce_fusion.1, bf16[3,32,512]{2,1,0:T(8,128)(2,1)S(1)} %collective-permute-done.5, pred[4]{0:T(512)(128)(4,1)S(1)} %get-tuple-element.56, pred[4]{0:T(512)(128)(4,1)S(1)} %get-tuple-element.53, pred[4]{0:T(512)(128)(4,1)S(1)} %get-tuple-element.50, ...), kind=kOutput, calls=%fused_computation.126 | convolution fusion | flops 4272128 | bytes 589836 | tf_op jit(solution)/shard_map/nab,nbr->nar/dot_general | solution.py:75
  70.6 1.8 %fusion.94 = f32[4,32,512]{2,1,0:T(8,128)} fusion(bf16[4,32,512]{2,1,0:T(8,128)(2,1)S(1)} %bitcast_reduce_fusion.1, bf16[3,32,512]{2,1,0:T(8,128)(2,1)S(1)} %collective-permute-done.4, pred[4]{0:T(512)(128)(4,1)S(1)} %get-tuple-element.55, pred[4]{0:T(512)(128)(4,1)S(1)} %get-tuple-element.52, pred[4]{0:T(512)(128)(4,1)S(1)} %get-tuple-element.49, ...), kind=kOutput, calls=%fused_computation.132 | convolution fusion | flops 4272128 | bytes 589836 | tf_op jit(solution)/shard_map/nab,nbr->nar/dot_general | solution.py:75
  72.5 2.4 %fusion.70 = f32[16,32,512]{2,1,0:T(8,128)} fusion(bf16[16,32,512]{2,1,0:T(8,128)(2,1)S(1)} %convolution_convert_fusion, bf16[3,32,512]{2,1,0:T(8,128)(2,1)S(1)} %collective-permute-done, pred[16]{0:T(512)(128)(4,1)S(1)} %copy-done.30, pred[16]{0:T(512)(128)(4,1)S(1)} %copy-done.29, pred[16]{0:T(512)(128)(4,1)S(1)} %copy-done.28, ...), kind=kOutput, calls=%fused_computation.96 | convolution fusion | flops 17088512 | bytes 2064432 | tf_op jit(solution)/shard_map/nab,nbr->nar/dot_general | solution.py:75
  74.9 3.6 %pad_maximum_fusion = (bf16[4096,512]{1,0:T(8,128)(2,1)}, bf16[4096,512]{1,0:T(8,128)(2,1)}) fusion(bf16[256,512]{1,0:T(8,128)(2,1)S(1)} %collective-permute-done.7, bf16[4096,512]{1,0:T(8,128)(2,1)S(1)} %copy-done.1, bf16[256,512]{1,0:T(8,128)(2,1)S(1)} %collective-permute-done.6), kind=kLoop, calls=%fused_computation.7 | loop fusion | flops 16777216 | bytes 13107200 | tf_op jit(solution)/shard_map/concatenate | solution.py:12
  78.5 4.2 %all-to-all-done = bf16[8,16,4096]{2,1,0:T(8,128)(2,1)} async-done(((bf16[8,16,4096]{2,1,0:T(8,128)(2,1)}), bf16[8,16,4096]{2,1,0:T(8,128)(2,1)}, u32[]{:S(2)}, u32[]{:S(2)}) %all-to-all-start) | async-done | bytes 1048608 | tf_op jit(solution)/shard_map/all_to_all | solution.py:25
  86.6 1.5 slice.452
  89.1 1.6 slice.450
  90.7 1.8 %slice.448 = bf16[64,3072]{1,0:T(8,128)(2,1)} slice(bf16[128,4096]{1,0:T(8,128)(2,1)} %bitcast.50), slice={[64:128], [1024:4096]} | slice | bytes 786432 | tf_op jit(solution)/shard_map/slice | solution.py:105
  96.0 1.7 %copy.129 = bf16[64,32,32]{2,1,0:T(8,128)(2,1)S(1)} copy(bf16[64,32,32]{0,2,1:T(8,128)(2,1)} %bitcast.441) | data formatting | bytes 262144 | tf_op jit(solution)/shard_map/slice | solution.py:111
  99.4 1.3 gather_fusion.3
  100.7 1.4 gather_fusion.2
  102.1 1.5 gather_fusion.1
  103.6 2.0 %slice.396 = bf16[16,3,32,32]{3,2,1,0:T(8,128)(2,1)} reshape(bf16[16,3072]{1,0:T(8,128)(2,1)} %slice.452) | data formatting | bytes 196608 | tf_op jit(solution)/shard_map/slice | solution.py:105
  105.6 2.2 %copy.111 = bf16[64,3072]{0,1:T(8,128)(2,1)} copy(bf16[64,3072]{1,0:T(8,128)(2,1)} %slice.448) | data formatting | bytes 786432 | tf_op jit(solution)/shard_map/slice | solution.py:105
  107.9 2.4 %slice.391 = bf16[32,3,32,32]{3,2,1,0:T(8,128)(2,1)} reshape(bf16[32,3072]{1,0:T(8,128)(2,1)} %slice.450) | data formatting | bytes 393216 | tf_op jit(solution)/shard_map/slice | solution.py:105
  110.2 3.1 %copy.118 = bf16[64,3,32,32]{3,2,1,0:T(8,128)(2,1)} copy(bf16[64,3,32,32]{0,3,2,1:T(8,128)(2,1)} %bitcast.438) | data formatting | bytes 786432 | tf_op jit(solution)/shard_map/slice | solution.py:105
  113.3 1.3 gather_fusion.4
  114.6 1.2 fusion.56
  115.8 1.2 convolution_bitcast_fusion.6
  117.1 1.0 fusion.55
  118.1 1.4 convolution_bitcast_fusion.5
  119.8 1.6 convolution_bitcast_fusion.4
  121.7 1.9 %convolution_bitcast_fusion.2 = f32[64,32,16]{1,2,0:T(8,128)S(1)} fusion(bf16[64,3,32,32]{3,2,1,0:T(8,128)(2,1)S(1)} %copy-done.3, bf16[64,3,32,16]{2,3,1,0:T(8,128)(2,1)} %bitcast.437, pred[64,3]{1,0:T(8,128)(4,1)S(1)} %copy-done.17), kind=kOutput, calls=%fused_computation.53 | convolution fusion | flops 6389760 | bytes 721088 | tf_op jit(solution)/shard_map/nsab,nsbr->nar/dot_general | solution.py:54
  124.8 6.3 %all-to-all-start.2 = ((bf16[32,2,512]{2,1,0:T(2,128)(2,1)}), bf16[32,2,512]{2,1,0:T(2,128)(2,1)S(1)}, u32[]{:S(2)}, u32[]{:S(2)}) async-start(bf16[32,2,512]{2,1,0:T(2,128)(2,1)} %reshape.480), calls=%async_computation.2 | async-start | bytes 131072 | tf_op jit(solution)/shard_map/all_to_all | solution.py:159
  131.2 8.6 %fusion.3 = f32[16,256,512]{2,1,0:T(8,128)} fusion(bf16[16,256,512]{2,1,0:T(8,128)(2,1)} %bitcast.436, pred[16]{0:T(512)(128)(4,1)S(1)} %copy-done.37, pred[16]{0:T(512)(128)(4,1)S(1)} %copy-done.38, pred[16]{0:T(512)(128)(4,1)S(1)} %copy-done.39, bf16[16,3,256,256]{3,2,1,0:T(8,128)(2,1)} %param.12), kind=kOutput, calls=%fused_computation.14 | convolution fusion | flops 1076887552 | bytes 18874416 | tf_op jit(solution)/shard_map/npq,nqr->npr/dot_general | solution.py:143
  141.2 1.4 fusion.53
  142.7 1.0 convolution_bitcast_fusion.1
  143.8 1.6 fusion.48
  145.5 1.2 convolution_bitcast_fusion
  146.7 6.6 %fusion.46 = f32[16,512,256]{1,2,0:T(8,128)} fusion(bf16[16,256,32]{1,2,0:T(8,128)(2,1)S(1)} %copy-done, f32[16,32,512]{2,1,0:T(8,128)S(1)} %convolution_bitcast_fusion, f32[16,32,512]{2,1,0:T(8,128)S(1)} %fusion.68, f32[16,32,512]{2,1,0:T(8,128)} %fusion.63, f32[16,32,512]{2,1,0:T(8,128)} %fusion.70, bf16[3,32,512]{2,1,0:T(8,128)(2,1)S(1)} %copy-done.7, ...), kind=kOutput, calls=%fused_computation.58 | convolution fusion | flops 152616960 | bytes 13860912 | tf_op jit(solution)/shard_map/npk,nkr->npr/dot_general | solution.py:168
  153.3 15.3 %fusion = bf16[16,256,512]{2,1,0:T(8,128)(2,1)} fusion(f32[16,512,256]{1,2,0:T(8,128)} %fusion.46, f32[16,256,512]{2,1,0:T(8,128)} %fusion.3, f32[16,256,512]{2,1,0:T(8,128)} %fusion.7, bf16[16,256,512]{2,1,0:T(8,128)(2,1)} %bitcast.435, pred[16]{0:T(512)(128)(4,1)S(1)} %copy-done.36, pred[16]{0:T(512)(128)(4,1)S(1)} %copy-done.35, ...), kind=kOutput, calls=%fused_computation.6 | convolution fusion | flops 1085276160 | bytes 39845936 | tf_op jit(solution)/shard_map/npq,nqr->npr/dot_general | solution.py:143
  (191 shorter events, 29.5 us)
Async XLA Ops:
  0.0 146.6 %copy-start = (bf16[16,256,32]{1,2,0:T(8,128)(2,1)S(1)}, bf16[16,256,32]{1,2,0:T(8,128)(2,1)}, u32[]{:S(2)}) copy-start(bf16[16,256,32]{1,2,0:T(8,128)(2,1)} %param.15) | copy-start | bytes 786436
  0.0 7.1 %copy-start.5 = (bf16[28,32,32]{2,1,0:T(8,128)(2,1)S(1)}, bf16[28,32,32]{2,1,0:T(8,128)(2,1)}, u32[]{:S(2)}) copy-start(bf16[28,32,32]{2,1,0:T(8,128)(2,1)} %param.16) | copy-start | bytes 172036
  0.0 24.3 %copy-start.13 = (s32[128,3]{0,1:T(4,128)S(1)}, s32[128,3]{0,1:T(4,128)}, u32[]{:S(2)}) copy-start(s32[128,3]{0,1:T(4,128)} %param.21) | copy-start | bytes 4612
  0.0 28.8 %copy-start.16 = (s32[28,3]{0,1:T(4,128)S(1)}, s32[28,3]{0,1:T(4,128)}, u32[]{:S(2)}) copy-start(s32[28,3]{0,1:T(4,128)} %param.20) | copy-start | bytes 1012
  0.0 31.2 %copy-start.24 = (s32[16,3]{0,1:T(4,128)S(1)}, s32[16,3]{0,1:T(4,128)}, u32[]{:S(2)}) copy-start(s32[16,3]{0,1:T(4,128)} %param.13) | copy-start | bytes 580
  0.0 36.1 %copy-start.14 = (bf16[16,32,32]{2,1,0:T(8,128)(2,1)S(1)}, bf16[16,32,32]{2,1,0:T(8,128)(2,1)}, u32[]{:S(2)}) copy-start(bf16[16,32,32]{2,1,0:T(8,128)(2,1)} %param.17) | copy-start | bytes 98308
  0.0 36.3 %copy-start.12 = (bf16[16,3,32,32]{3,2,1,0:T(8,128)(2,1)S(1)}, bf16[16,3,32,32]{3,2,1,0:T(8,128)(2,1)}, u32[]{:S(2)}) copy-start(bf16[16,3,32,32]{3,2,1,0:T(8,128)(2,1)} %param.19) | copy-start | bytes 294916
  3.9 68.6 %collective-permute-start = (bf16[3,32,512]{2,1,0:T(8,128)(2,1)}, bf16[3,32,512]{2,1,0:T(8,128)(2,1)S(1)}, u32[]{:S(2)}, u32[]{:S(2)}) collective-permute-start(bf16[3,32,512]{2,1,0:T(8,128)(2,1)} %get-tuple-element.9), channel_id=1, source_target_pairs={{0,8},{8,16},{16,24},{24,32},{32,40},{40,48},{48,56},{56,64},{64,7... | collective-permute-start | bytes 294920 | tf_op jit(solution)/shard_map/ppermute | solution.py:14
  6.5 50.9 %collective-permute-start.1 = (bf16[3,32,512]{2,1,0:T(8,128)(2,1)S(1)}, bf16[3,32,512]{2,1,0:T(8,128)(2,1)S(1)}, u32[]{:S(2)}, u32[]{:S(2)}) collective-permute-start(bf16[3,32,512]{2,1,0:T(8,128)(2,1)S(1)} %get-tuple-element.10), channel_id=1, source_target_pairs={{8,0},{16,8},{24,16},{32,24},{40,32},{48,40},{56,48},{64,56},{72,6... | collective-permute-start | bytes 294920 | tf_op jit(solution)/shard_map/ppermute | solution.py:16
  9.0 36.5 %all-to-all-start.1 = ((bf16[32,2,512]{2,1,0:T(2,128)(2,1)}), bf16[32,2,512]{2,1,0:T(2,128)(2,1)S(1)}, u32[]{:S(2)}, u32[]{:S(2)}) async-start(bf16[32,2,512]{2,1,0:T(2,128)(2,1)} %reshape.478), calls=%async_computation.1 | async-start | bytes 131072 | tf_op jit(solution)/shard_map/all_to_all | solution.py:157
  18.2 52.4 %collective-permute-start.4 = (bf16[3,32,512]{2,1,0:T(8,128)(2,1)}, bf16[3,32,512]{2,1,0:T(8,128)(2,1)S(1)}, u32[]{:S(2)}, u32[]{:S(2)}) collective-permute-start(bf16[3,32,512]{2,1,0:T(8,128)(2,1)} %get-tuple-element.13), channel_id=1, source_target_pairs={{0,8},{8,16},{16,24},{24,32},{32,40},{40,48},{48,56},{56,64},{64,7... | collective-permute-start | bytes 294920 | tf_op jit(solution)/shard_map/ppermute | solution.py:14
  19.8 44.9 %collective-permute-start.5 = (bf16[3,32,512]{2,1,0:T(8,128)(2,1)}, bf16[3,32,512]{2,1,0:T(8,128)(2,1)S(1)}, u32[]{:S(2)}, u32[]{:S(2)}) collective-permute-start(bf16[3,32,512]{2,1,0:T(8,128)(2,1)} %get-tuple-element.14), channel_id=1, source_target_pairs={{8,0},{16,8},{24,16},{32,24},{40,32},{48,40},{56,48},{64,56},{72,6... | collective-permute-start | bytes 294920 | tf_op jit(solution)/shard_map/ppermute | solution.py:16
  20.5 34.8 %collective-permute-start.3 = (bf16[3,32,512]{2,1,0:T(8,128)(2,1)S(1)}, bf16[3,32,512]{2,1,0:T(8,128)(2,1)S(1)}, u32[]{:S(2)}, u32[]{:S(2)}) collective-permute-start(bf16[3,32,512]{2,1,0:T(8,128)(2,1)S(1)} %get-tuple-element.12), channel_id=1, source_target_pairs={{8,0},{16,8},{24,16},{32,24},{40,32},{48,40},{56,48},{64,56},{72,6... | collective-permute-start | bytes 294920 | tf_op jit(solution)/shard_map/ppermute | solution.py:16
  45.5 12.6 %copy-start.31 = (pred[16]{0:T(512)(128)(4,1)S(1)}, pred[16]{0:T(512)(128)(4,1)}, u32[]{:S(2)}) copy-start(pred[16]{0:T(512)(128)(4,1)} %get-tuple-element.27) | copy-start | bytes 52
  45.5 12.6 %copy-start.32 = (pred[16]{0:T(512)(128)(4,1)S(1)}, pred[16]{0:T(512)(128)(4,1)}, u32[]{:S(2)}) copy-start(pred[16]{0:T(512)(128)(4,1)} %get-tuple-element.30) | copy-start | bytes 52
  45.5 12.6 %copy-start.33 = (pred[16]{0:T(512)(128)(4,1)S(1)}, pred[16]{0:T(512)(128)(4,1)}, u32[]{:S(2)}) copy-start(pred[16]{0:T(512)(128)(4,1)} %get-tuple-element.33) | copy-start | bytes 52
  46.6 13.1 %copy-start.40 = (pred[8]{0:T(512)(128)(4,1)S(1)}, pred[8]{0:T(512)(128)(4,1)}, u32[]{:S(2)}) copy-start(pred[8]{0:T(512)(128)(4,1)} %get-tuple-element.38) | copy-start | bytes 28
  46.6 13.1 %copy-start.41 = (pred[8]{0:T(512)(128)(4,1)S(1)}, pred[8]{0:T(512)(128)(4,1)}, u32[]{:S(2)}) copy-start(pred[8]{0:T(512)(128)(4,1)} %get-tuple-element.41) | copy-start | bytes 28
  46.6 13.1 %copy-start.42 = (pred[8]{0:T(512)(128)(4,1)S(1)}, pred[8]{0:T(512)(128)(4,1)}, u32[]{:S(2)}) copy-start(pred[8]{0:T(512)(128)(4,1)} %get-tuple-element.44) | copy-start | bytes 28
  46.6 36.1 %all-to-all-start = ((bf16[8,16,4096]{2,1,0:T(8,128)(2,1)}), bf16[8,16,4096]{2,1,0:T(8,128)(2,1)}, u32[]{:S(2)}, u32[]{:S(2)}) async-start(bf16[8,16,4096]{2,1,0:T(8,128)(2,1)} %broadcast_in_dim.421), calls=%async_computation | async-start | bytes 2097152 | tf_op jit(solution)/shard_map/all_to_all | solution.py:25
  53.6 12.9 %copy-start.43 = (pred[16]{0:T(512)(128)(4,1)S(1)}, pred[16]{0:T(512)(128)(4,1)}, u32[]{:S(2)}) copy-start(pred[16]{0:T(512)(128)(4,1)} %get-tuple-element.26) | copy-start | bytes 52
  53.6 12.9 %copy-start.44 = (pred[16]{0:T(512)(128)(4,1)S(1)}, pred[16]{0:T(512)(128)(4,1)}, u32[]{:S(2)}) copy-start(pred[16]{0:T(512)(128)(4,1)} %get-tuple-element.29) | copy-start | bytes 52
  53.6 12.9 %copy-start.45 = (pred[16]{0:T(512)(128)(4,1)S(1)}, pred[16]{0:T(512)(128)(4,1)}, u32[]{:S(2)}) copy-start(pred[16]{0:T(512)(128)(4,1)} %get-tuple-element.32) | copy-start | bytes 52
  55.3 17.2 %copy-start.28 = (pred[16]{0:T(512)(128)(4,1)S(1)}, pred[16]{0:T(512)(128)(4,1)}, u32[]{:S(2)}) copy-start(pred[16]{0:T(512)(128)(4,1)} %get-tuple-element.25) | copy-start | bytes 52
  55.3 17.2 %copy-start.29 = (pred[16]{0:T(512)(128)(4,1)S(1)}, pred[16]{0:T(512)(128)(4,1)}, u32[]{:S(2)}) copy-start(pred[16]{0:T(512)(128)(4,1)} %get-tuple-element.28) | copy-start | bytes 52
  55.3 17.2 %copy-start.30 = (pred[16]{0:T(512)(128)(4,1)S(1)}, pred[16]{0:T(512)(128)(4,1)}, u32[]{:S(2)}) copy-start(pred[16]{0:T(512)(128)(4,1)} %get-tuple-element.31) | copy-start | bytes 52
  55.3 6.4 %collective-permute-start.2 = (bf16[3,32,512]{2,1,0:T(8,128)(2,1)}, bf16[3,32,512]{2,1,0:T(8,128)(2,1)S(1)}, u32[]{:S(2)}, u32[]{:S(2)}) collective-permute-start(bf16[3,32,512]{2,1,0:T(8,128)(2,1)} %get-tuple-element.11), channel_id=1, source_target_pairs={{0,8},{8,16},{16,24},{24,32},{32,40},{40,48},{48,56},{56,64},{64,7... | collective-permute-start | bytes 294920 | tf_op jit(solution)/shard_map/ppermute | solution.py:14
  57.4 17.5 %collective-permute-start.7 = (bf16[256,512]{1,0:T(8,128)(2,1)}, bf16[256,512]{1,0:T(8,128)(2,1)S(1)}, u32[]{:S(2)}, u32[]{:S(2)}) collective-permute-start(bf16[256,512]{1,0:T(8,128)(2,1)} %get-tuple-element.7), channel_id=1, source_target_pairs={{8,0},{16,8},{24,16},{32,24},{40,32},{48,40},{56,48},{64,56},{72,6... | collective-permute-start | bytes 786440 | tf_op jit(solution)/shard_map/ppermute | solution.py:16
  58.0 16.8 %copy-start.1 = (bf16[4096,512]{1,0:T(8,128)(2,1)S(1)}, bf16[4096,512]{1,0:T(8,128)(2,1)}, u32[]{:S(2)}) copy-start(bf16[4096,512]{1,0:T(8,128)(2,1)} %param.11) | copy-start | bytes 12582916
  61.7 16.8 %copy-start.8 = (bf16[3,32,512]{2,1,0:T(8,128)(2,1)}, bf16[3,32,512]{2,1,0:T(8,128)(2,1)S(1)}, u32[]{:S(2)}) copy-start(bf16[3,32,512]{2,1,0:T(8,128)(2,1)S(1)} %collective-permute-done.2) | copy-start | bytes 294916
  61.7 13.2 %collective-permute-start.6 = (bf16[256,512]{1,0:T(8,128)(2,1)S(1)}, bf16[256,512]{1,0:T(8,128)(2,1)S(1)}, u32[]{:S(2)}, u32[]{:S(2)}) collective-permute-start(bf16[256,512]{1,0:T(8,128)(2,1)S(1)} %get-tuple-element.8), channel_id=1, source_target_pairs={{0,8},{8,16},{16,24},{24,32},{32,40},{40,48},{48,56},{56,64},{64,7... | collective-permute-start | bytes 786440 | tf_op jit(solution)/shard_map/ppermute | solution.py:14
  70.6 7.9 %copy-start.10 = (bf16[3,32,512]{2,1,0:T(8,128)(2,1)}, bf16[3,32,512]{2,1,0:T(8,128)(2,1)S(1)}, u32[]{:S(2)}) copy-start(bf16[3,32,512]{2,1,0:T(8,128)(2,1)S(1)} %collective-permute-done.4) | copy-start | bytes 294916
  103.6 16.1 %copy-start.4 = (bf16[96,32,16]{1,2,0:T(8,128)(2,1)S(1)}, bf16[96,32,16]{1,2,0:T(8,128)(2,1)}, u32[]{:S(2)}) copy-start(bf16[96,32,16]{1,2,0:T(8,128)(2,1)} %gather_fusion.1) | copy-start | bytes 294916
  114.6 7.0 %copy-start.3 = (bf16[64,3,32,32]{3,2,1,0:T(8,128)(2,1)S(1)}, bf16[64,3,32,32]{3,2,1,0:T(8,128)(2,1)}, u32[]{:S(2)}) copy-start(bf16[64,3,32,32]{3,2,1,0:T(8,128)(2,1)} %copy.118) | copy-start | bytes 1179652
  114.6 7.0 %copy-start.17 = (pred[64,3]{1,0:T(8,128)(4,1)S(1)}, pred[64,3]{1,0:T(8,128)(4,1)}, u32[]{:S(2)}) copy-start(pred[64,3]{1,0:T(8,128)(4,1)} %copy.112) | copy-start | bytes 580
  119.5 11.6 %copy-start.37 = (pred[16]{0:T(512)(128)(4,1)S(1)}, pred[16]{0:T(512)(128)(4,1)}, u32[]{:S(2)}) copy-start(pred[16]{0:T(512)(128)(4,1)} %get-tuple-element.21) | copy-start | bytes 52
  119.5 11.6 %copy-start.38 = (pred[16]{0:T(512)(128)(4,1)S(1)}, pred[16]{0:T(512)(128)(4,1)}, u32[]{:S(2)}) copy-start(pred[16]{0:T(512)(128)(4,1)} %get-tuple-element.22) | copy-start | bytes 52
  119.6 11.6 %copy-start.39 = (pred[16]{0:T(512)(128)(4,1)S(1)}, pred[16]{0:T(512)(128)(4,1)}, u32[]{:S(2)}) copy-start(pred[16]{0:T(512)(128)(4,1)} %get-tuple-element.23) | copy-start | bytes 52
  124.8 15.0 %all-to-all-start.2 = ((bf16[32,2,512]{2,1,0:T(2,128)(2,1)}), bf16[32,2,512]{2,1,0:T(2,128)(2,1)S(1)}, u32[]{:S(2)}, u32[]{:S(2)}) async-start(bf16[32,2,512]{2,1,0:T(2,128)(2,1)} %reshape.480), calls=%async_computation.2 | async-start | bytes 131072 | tf_op jit(solution)/shard_map/all_to_all | solution.py:159
  131.1 10.1 %copy-start.11 = (bf16[3,32,512]{2,1,0:T(8,128)(2,1)S(1)}, bf16[3,32,512]{2,1,0:T(8,128)(2,1)}, u32[]{:S(2)}) copy-start(bf16[3,32,512]{2,1,0:T(8,128)(2,1)} %copy-done.10) | copy-start | bytes 294916
  131.1 10.1 %copy-start.21 = (pred[4]{0:T(512)(128)(4,1)S(1)}, pred[4]{0:T(512)(128)(4,1)}, u32[]{:S(2)}) copy-start(pred[4]{0:T(512)(128)(4,1)} %get-tuple-element.48) | copy-start | bytes 16
  131.1 10.1 %copy-start.22 = (pred[4]{0:T(512)(128)(4,1)S(1)}, pred[4]{0:T(512)(128)(4,1)}, u32[]{:S(2)}) copy-start(pred[4]{0:T(512)(128)(4,1)} %get-tuple-element.58) | copy-start | bytes 16
  131.1 10.1 %copy-start.23 = (pred[4]{0:T(512)(128)(4,1)S(1)}, pred[4]{0:T(512)(128)(4,1)}, u32[]{:S(2)}) copy-start(pred[4]{0:T(512)(128)(4,1)} %get-tuple-element.59) | copy-start | bytes 16
  140.2 6.5 %copy-start.7 = (bf16[3,32,512]{2,1,0:T(8,128)(2,1)S(1)}, bf16[3,32,512]{2,1,0:T(8,128)(2,1)}, u32[]{:S(2)}) copy-start(bf16[3,32,512]{2,1,0:T(8,128)(2,1)} %copy-done.6) | copy-start | bytes 294916
  140.2 6.5 %copy-start.18 = (pred[16]{0:T(512)(128)(4,1)S(1)}, pred[16]{0:T(512)(128)(4,1)}, u32[]{:S(2)}) copy-start(pred[16]{0:T(512)(128)(4,1)} %get-tuple-element.24) | copy-start | bytes 52
  146.7 6.6 %copy-start.34 = (pred[16]{0:T(512)(128)(4,1)S(1)}, pred[16]{0:T(512)(128)(4,1)}, u32[]{:S(2)}) copy-start(pred[16]{0:T(512)(128)(4,1)} %get-tuple-element.15) | copy-start | bytes 52
  146.7 6.6 %copy-start.35 = (pred[16]{0:T(512)(128)(4,1)S(1)}, pred[16]{0:T(512)(128)(4,1)}, u32[]{:S(2)}) copy-start(pred[16]{0:T(512)(128)(4,1)} %get-tuple-element.18) | copy-start | bytes 52
  146.7 6.6 %copy-start.36 = (pred[16]{0:T(512)(128)(4,1)S(1)}, pred[16]{0:T(512)(128)(4,1)}, u32[]{:S(2)}) copy-start(pred[16]{0:T(512)(128)(4,1)} %get-tuple-element.20) | copy-start | bytes 52
  (9 other events, 39.4 us)
where the time goes:
time: 170 us; the launch traced here: 169 us
  matrix products  77.7 us (46%)
  local copies, waits for them, and re-layouts  44.4 us (26%)
  starting transfers between devices  32 us (19%)
  other arithmetic  9.4 us (6%)
  waiting for transfers between devices  4.23 us (2%)
    dot_general x3, matrix products, body(): jnp.einsum('npq,nqr->npr', chosen, shifted, preferred_element_type=jnp.fl...  32.6 us
    dot_general x11, matrix products, couple_window(): jnp.einsum('nab,nbr->nar', chosen, shifted, preferred_element_type=jnp.fl...  20.6 us
    slice x11, local copies, waits for them, and re-layouts, coarse_pass(): couple_all[clusters:2 * clusters]  17.8 us
    all_to_all x1, starting transfers between devices, body(): lax.all_to_all(moments, 'rows', split_axis=2, concat_axis=0, tiled=True)  8.54 us
    dot_general x5, matrix products, couple_masked(): jnp.einsum('nsab,nsbr->nar', blocks, picked, preferred_element_type=jnp.f...  7.33 us
    gather x5, local copies, waits for them, and re-layouts, couple_masked(): picked = moments[jnp.maximum(partners, 0)]  7.18 us
    slice x9, local copies, waits for them, and re-layouts, coarse_pass(): downward = lower(downward, transfer_all[clusters:2 * clusters], coupled)  6.86 us
    all_to_all x1, starting transfers between devices, from_everyone(): return lax.all_to_all(copies, axis, split_axis=0, concat_axis=0, tiled=True)  6.79 us
  transfers between devices with their start and end apart: 11, of which 1 were waited for; matrix products, arithmetic and copies ran while one was open for 34% of the time, Pallas kernels for 0%

commit v1 on v0

--- a/solution.py
+++ b/solution.py
@@ -154,7 +154,10 @@
         moments = lift(moments, transfer_fine[firsts[level] : firsts[level] + level_counts[level]])
         upward.append(moments)
     tables = sent_together((transfer_coarse, couple_coarse), "rhs", 0, 1)
-    columns = lax.all_to_all(moments, "rows", split_axis=2, concat_axis=0, tiled=True)
+    columns = jnp.concatenate(
+        lax.all_to_all(jnp.stack(jnp.split(moments, lax.axis_size("rows"), axis=2)), "rows", 0, 0),
+        axis=0,
+    )
     result = coarse_pass(columns, tables[0], tables[1], far_coarse)
     parents = lax.all_to_all(result, "rows", split_axis=0, concat_axis=2, tiled=True)
     downward = parents

time: 170 us -> 172 us (1.012)
  local copies, waits for them, and re-layouts: 44.4 us -> 46.8 us
  starting transfers between devices: 32 us -> 33.9 us
    all_to_all x1, starting transfers between devices: 8.54 us -> 3.63 us  [body(): lax.all_to_all(jnp.stack(jnp.split(moments, lax.axis_size('rows'), axis=2...]
    ppermute x4, starting transfers between devices: 5.03 us -> 9.68 us  [padded_2(): lax.ppermute(head, axis, [((i + 1) % count, i) for i in range(count)])]
    unnamed x96 -> x103, local copies, waits for them, and re-layouts: 2.25 us -> 5.18 us
where the time goes in v1:
time: 172 us; the launch traced here: 170 us
  matrix products  77.5 us (45%)
  local copies, waits for them, and re-layouts  46.8 us (27%)
  starting transfers between devices  33.9 us (20%)
  other arithmetic  8.18 us (5%)
  waiting for transfers between devices  2.83 us (2%)
    dot_general x3, matrix products, body(): jnp.einsum('npq,nqr->npr', chosen, shifted, preferred_element_type=jnp.fl...  32.6 us
    dot_general x11, matrix products, couple_window(): jnp.einsum('nab,nbr->nar', chosen, shifted, preferred_element_type=jnp.fl...  20.5 us
    slice x11, local copies, waits for them, and re-layouts, coarse_pass(): couple_all[clusters:2 * clusters]  17.8 us
    ppermute x4, starting transfers between devices, padded_2(): lax.ppermute(head, axis, [((i + 1) % count, i) for i in range(count)])  9.68 us
    all_to_all x1, starting transfers between devices, body(): lax.all_to_all(result, 'rows', split_axis=0, concat_axis=2, tiled=True)  7.48 us
    dot_general x5, matrix products, couple_masked(): jnp.einsum('nsab,nsbr->nar', blocks, picked, preferred_element_type=jnp.f...  7.33 us
    gather x5, local copies, waits for them, and re-layouts, couple_masked(): picked = moments[jnp.maximum(partners, 0)]  7.21 us
    slice x9, local copies, waits for them, and re-layouts, coarse_pass(): downward = lower(downward, transfer_all[clusters:2 * clusters], coupled)  6.87 us
  transfers between devices with their start and end apart: 11, of which 1 were waited for; matrix products, arithmetic and copies ran while one was open for 34% of the time, Pallas kernels for 0%

profile of v1, /device:TPU:1, one launch (start us, length us, event | category | flops | bytes accessed | tf_op | source)
XLA Modules:
  0.0 170.0 jit_solution(18112974687398505836)
XLA Ops:
  0.0 3.1 %convolution_convert_fusion = bf16[16,32,512]{2,1,0:T(8,128)(2,1)S(1)} fusion(bf16[16,256,32]{1,2,0:T(8,128)(2,1)} %param.14, bf16[16,256,512]{2,1,0:T(8,128)(2,1)} %bitcast.556), kind=kOutput, calls=%fused_computation.51 | convolution fusion | flops 134479872 | bytes 4980736 | tf_op jit(solution)/shard_map/npk,npr->nkr/dot_general | solution.py:147
  3.2 2.7 %collective-permute-start = (bf16[3,32,512]{2,1,0:T(8,128)(2,1)S(1)}, bf16[3,32,512]{2,1,0:T(8,128)(2,1)S(1)}, u32[]{:S(2)}, u32[]{:S(2)}) collective-permute-start(bf16[3,32,512]{2,1,0:T(8,128)(2,1)S(1)} %get-tuple-element.9), channel_id=1, source_target_pairs={{0,8},{8,16},{16,24},{24,32},{32,40},{40,48},{48,56},{56,64},{64,7... | collective-permute-start | bytes 294920 | tf_op jit(solution)/shard_map/ppermute | solution.py:14
  7.9 1.1 collective-permute-start.4
  9.0 3.9 %collective-permute-start.5 = (bf16[3,32,512]{2,1,0:T(8,128)(2,1)}, bf16[3,32,512]{2,1,0:T(8,128)(2,1)S(1)}, u32[]{:S(2)}, u32[]{:S(2)}) collective-permute-start(bf16[3,32,512]{2,1,0:T(8,128)(2,1)} %get-tuple-element.14), channel_id=1, source_target_pairs={{8,0},{16,8},{24,16},{32,24},{40,32},{48,40},{56,48},{64,56},{72,6... | collective-permute-start | bytes 294920 | tf_op jit(solution)/shard_map/ppermute | solution.py:16
  13.5 5.1 %collective-permute-start.3 = (bf16[3,32,512]{2,1,0:T(8,128)(2,1)S(1)}, bf16[3,32,512]{2,1,0:T(8,128)(2,1)S(1)}, u32[]{:S(2)}, u32[]{:S(2)}) collective-permute-start(bf16[3,32,512]{2,1,0:T(8,128)(2,1)S(1)} %get-tuple-element.12), channel_id=1, source_target_pairs={{8,0},{16,8},{24,16},{32,24},{40,32},{48,40},{56,48},{64,56},{72,6... | collective-permute-start | bytes 294920 | tf_op jit(solution)/shard_map/ppermute | solution.py:16
  22.4 3.6 %all-to-all-start.1 = ((bf16[32,2,512]{2,1,0:T(2,128)(2,1)}), bf16[32,2,512]{2,1,0:T(2,128)(2,1)S(1)}, u32[]{:S(2)}, u32[]{:S(2)}) async-start(bf16[32,2,512]{2,1,0:T(2,128)(2,1)} %reshape.482), calls=%async_computation.1 | async-start | bytes 131072 | tf_op jit(solution)/shard_map/all_to_all | solution.py:158
  26.8 1.8 %fusion.297 = (bf16[256,512]{1,0:T(8,128)(2,1)}, bf16[256,512]{1,0:T(8,128)(2,1)}) fusion(bf16[4096,512]{1,0:T(8,128)(2,1)} %param.11), kind=kLoop, calls=%fused_computation.468 | loop fusion | bytes 1048576 | tf_op jit(solution)/shard_map/slice | solution.py:10
  37.3 8.7 %fusion.7 = f32[16,256,512]{2,1,0:T(8,128)} fusion(bf16[16,256,512]{2,1,0:T(8,128)(2,1)} %bitcast.557, pred[16]{0:T(512)(128)(4,1)S(1)} %get-tuple-element.19, pred[16]{0:T(512)(128)(4,1)S(1)} %get-tuple-element.17, pred[16]{0:T(512)(128)(4,1)S(1)} %get-tuple-element.16, bf16[16,3,256,256]{3,2,1,0:T(8,128)(2,1)} %param.12), kind=kOutput, calls=%fused_computation.17 | convolution fusion | flops 1076887552 | bytes 18874416 | tf_op jit(solution)/shard_map/npq,nqr->npr/dot_general | solution.py:143
  46.0 1.1 broadcast_in_dim.421
  47.1 6.5 %all-to-all-start = ((bf16[8,16,4096]{2,1,0:T(8,128)(2,1)}), bf16[8,16,4096]{2,1,0:T(8,128)(2,1)}, u32[]{:S(2)}, u32[]{:S(2)}) async-start(bf16[8,16,4096]{2,1,0:T(8,128)(2,1)} %broadcast_in_dim.421), calls=%async_computation | async-start | bytes 2097152 | tf_op jit(solution)/shard_map/all_to_all | solution.py:25
  53.7 1.6 gather_fusion
  55.4 1.8 %collective-permute-start.2 = (bf16[3,32,512]{2,1,0:T(8,128)(2,1)}, bf16[3,32,512]{2,1,0:T(8,128)(2,1)S(1)}, u32[]{:S(2)}, u32[]{:S(2)}) collective-permute-start(bf16[3,32,512]{2,1,0:T(8,128)(2,1)} %get-tuple-element.11), channel_id=1, source_target_pairs={{0,8},{8,16},{16,24},{24,32},{32,40},{40,48},{48,56},{56,64},{64,7... | collective-permute-start | bytes 294920 | tf_op jit(solution)/shard_map/ppermute | solution.py:14
  57.2 2.0 %fusion.80 = f32[8,32,512]{2,1,0:T(8,128)} fusion(bf16[3,32,512]{2,1,0:T(8,128)(2,1)S(1)} %collective-permute-done.3, bf16[8,32,512]{2,1,0:T(8,128)(2,1)S(1)} %bitcast_reduce_fusion, pred[8]{0:T(512)(128)(4,1)S(1)} %get-tuple-element.45, pred[8]{0:T(512)(128)(4,1)S(1)} %get-tuple-element.42, pred[8]{0:T(512)(128)(4,1)S(1)} %get-tuple-element.39, ...), kind=kOutput, calls=%fused_computation.111 | convolution fusion | flops 8544256 | bytes 1081368 | tf_op jit(solution)/shard_map/nab,nbr->nar/dot_general | solution.py:75
  59.8 1.6 fusion.68
  61.4 2.0 %fusion.76 = f32[8,32,512]{2,1,0:T(8,128)} fusion(bf16[8,32,512]{2,1,0:T(8,128)(2,1)S(1)} %bitcast_reduce_fusion, bf16[3,32,512]{2,1,0:T(8,128)(2,1)S(1)} %collective-permute-done.3, pred[8]{0:T(512)(128)(4,1)S(1)} %get-tuple-element.44, pred[8]{0:T(512)(128)(4,1)S(1)} %get-tuple-element.41, pred[8]{0:T(512)(128)(4,1)S(1)} %get-tuple-element.38, ...), kind=kOutput, calls=%fused_computation.108 | convolution fusion | flops 8544256 | bytes 1081368 | tf_op jit(solution)/shard_map/nab,nbr->nar/dot_general | solution.py:75
  63.4 1.1 collective-permute-start.6
  64.5 2.0 %fusion.82 = f32[8,32,512]{2,1,0:T(8,128)} fusion(bf16[8,32,512]{2,1,0:T(8,128)(2,1)S(1)} %bitcast_reduce_fusion, bf16[3,32,512]{2,1,0:T(8,128)(2,1)S(1)} %collective-permute-done.2, pred[8]{0:T(512)(128)(4,1)S(1)} %get-tuple-element.43, pred[8]{0:T(512)(128)(4,1)S(1)} %get-tuple-element.40, pred[8]{0:T(512)(128)(4,1)S(1)} %get-tuple-element.37, ...), kind=kOutput, calls=%fused_computation.114 | convolution fusion | flops 8544256 | bytes 1081368 | tf_op jit(solution)/shard_map/nab,nbr->nar/dot_general | solution.py:75
  66.5 1.7 %fusion.92 = f32[4,32,512]{2,1,0:T(8,128)} fusion(bf16[3,32,512]{2,1,0:T(8,128)(2,1)S(1)} %collective-permute-done.5, bf16[4,32,512]{2,1,0:T(8,128)(2,1)S(1)} %bitcast_reduce_fusion.1, pred[4]{0:T(512)(128)(4,1)S(1)} %get-tuple-element.57, pred[4]{0:T(512)(128)(4,1)S(1)} %get-tuple-element.54, pred[4]{0:T(512)(128)(4,1)S(1)} %get-tuple-element.51, ...), kind=kOutput, calls=%fused_computation.129 | convolution fusion | flops 4272128 | bytes 589836 | tf_op jit(solution)/shard_map/nab,nbr->nar/dot_general | solution.py:75
  68.2 2.3 %fusion.63 = f32[16,32,512]{2,1,0:T(8,128)} fusion(bf16[16,32,512]{2,1,0:T(8,128)(2,1)S(1)} %convolution_convert_fusion, bf16[3,32,512]{2,1,0:T(8,128)(2,1)} %copy-done.15, pred[16]{0:T(512)(128)(4,1)S(1)} %get-tuple-element.32, pred[16]{0:T(512)(128)(4,1)S(1)} %get-tuple-element.29, pred[16]{0:T(512)(128)(4,1)S(1)} %get-tuple-element.26, ...), kind=kOutput, calls=%fused_computation.90 | convolution fusion | flops 17088512 | bytes 2064432 | tf_op jit(solution)/shard_map/nab,nbr->nar/dot_general | solution.py:75
  70.5 1.7 %fusion.88 = f32[4,32,512]{2,1,0:T(8,128)} fusion(bf16[4,32,512]{2,1,0:T(8,128)(2,1)S(1)} %bitcast_reduce_fusion.1, bf16[3,32,512]{2,1,0:T(8,128)(2,1)S(1)} %collective-permute-done.5, pred[4]{0:T(512)(128)(4,1)S(1)} %get-tuple-element.56, pred[4]{0:T(512)(128)(4,1)S(1)} %get-tuple-element.53, pred[4]{0:T(512)(128)(4,1)S(1)} %get-tuple-element.50, ...), kind=kOutput, calls=%fused_computation.126 | convolution fusion | flops 4272128 | bytes 589836 | tf_op jit(solution)/shard_map/nab,nbr->nar/dot_general | solution.py:75
  72.3 1.8 %fusion.94 = f32[4,32,512]{2,1,0:T(8,128)} fusion(bf16[4,32,512]{2,1,0:T(8,128)(2,1)S(1)} %bitcast_reduce_fusion.1, bf16[3,32,512]{2,1,0:T(8,128)(2,1)S(1)} %collective-permute-done.4, pred[4]{0:T(512)(128)(4,1)S(1)} %get-tuple-element.55, pred[4]{0:T(512)(128)(4,1)S(1)} %get-tuple-element.52, pred[4]{0:T(512)(128)(4,1)S(1)} %get-tuple-element.49, ...), kind=kOutput, calls=%fused_computation.132 | convolution fusion | flops 4272128 | bytes 589836 | tf_op jit(solution)/shard_map/nab,nbr->nar/dot_general | solution.py:75
  74.0 2.4 %fusion.70 = f32[16,32,512]{2,1,0:T(8,128)} fusion(bf16[16,32,512]{2,1,0:T(8,128)(2,1)S(1)} %convolution_convert_fusion, bf16[3,32,512]{2,1,0:T(8,128)(2,1)S(1)} %collective-permute-done, pred[16]{0:T(512)(128)(4,1)S(1)} %get-tuple-element.31, pred[16]{0:T(512)(128)(4,1)S(1)} %get-tuple-element.28, pred[16]{0:T(512)(128)(4,1)S(1)} %get-tuple-element.25, ...), kind=kOutput, calls=%fused_computation.96 | convolution fusion | flops 17088512 | bytes 2064432 | tf_op jit(solution)/shard_map/nab,nbr->nar/dot_general | solution.py:75
  76.4 3.6 %pad_maximum_fusion = (bf16[4096,512]{1,0:T(8,128)(2,1)}, bf16[4096,512]{1,0:T(8,128)(2,1)}) fusion(bf16[256,512]{1,0:T(8,128)(2,1)S(1)} %collective-permute-done.7, bf16[4096,512]{1,0:T(8,128)(2,1)S(1)} %copy-done.1, bf16[256,512]{1,0:T(8,128)(2,1)S(1)} %collective-permute-done.6), kind=kLoop, calls=%fused_computation.7 | loop fusion | flops 16777216 | bytes 13107200 | tf_op jit(solution)/shard_map/concatenate | solution.py:12
  80.1 2.8 %all-to-all-done = bf16[8,16,4096]{2,1,0:T(8,128)(2,1)} async-done(((bf16[8,16,4096]{2,1,0:T(8,128)(2,1)}), bf16[8,16,4096]{2,1,0:T(8,128)(2,1)}, u32[]{:S(2)}, u32[]{:S(2)}) %all-to-all-start) | async-done | bytes 1048608 | tf_op jit(solution)/shard_map/all_to_all | solution.py:25
  86.8 1.5 slice.452
  89.3 1.6 slice.450
  90.9 1.8 %slice.448 = bf16[64,3072]{1,0:T(8,128)(2,1)} slice(bf16[128,4096]{1,0:T(8,128)(2,1)} %bitcast.50), slice={[64:128], [1024:4096]} | slice | bytes 786432 | tf_op jit(solution)/shard_map/slice | solution.py:105
  96.2 1.7 %copy.157 = bf16[64,32,32]{2,1,0:T(8,128)(2,1)S(1)} copy(bf16[64,32,32]{0,2,1:T(8,128)(2,1)} %bitcast.567) | data formatting | bytes 262144 | tf_op jit(solution)/shard_map/slice | solution.py:111
  99.6 1.3 gather_fusion.3
  100.9 1.4 gather_fusion.2
  102.3 1.5 gather_fusion.1
  103.9 2.0 %slice.396 = bf16[16,3,32,32]{3,2,1,0:T(8,128)(2,1)} reshape(bf16[16,3072]{1,0:T(8,128)(2,1)} %slice.452) | data formatting | bytes 196608 | tf_op jit(solution)/shard_map/slice | solution.py:105
  105.9 2.2 %copy.141 = bf16[64,3072]{0,1:T(8,128)(2,1)} copy(bf16[64,3072]{1,0:T(8,128)(2,1)} %slice.448) | data formatting | bytes 786432 | tf_op jit(solution)/shard_map/slice | solution.py:105
  108.1 2.4 %slice.391 = bf16[32,3,32,32]{3,2,1,0:T(8,128)(2,1)} reshape(bf16[32,3072]{1,0:T(8,128)(2,1)} %slice.450) | data formatting | bytes 393216 | tf_op jit(solution)/shard_map/slice | solution.py:105
  110.5 3.1 %copy.146 = bf16[64,3,32,32]{3,2,1,0:T(8,128)(2,1)} copy(bf16[64,3,32,32]{0,3,2,1:T(8,128)(2,1)} %bitcast.563) | data formatting | bytes 786432 | tf_op jit(solution)/shard_map/slice | solution.py:105
  113.5 1.3 gather_fusion.4
  114.8 1.2 fusion.56
  116.1 1.2 convolution_bitcast_fusion.6
  118.3 1.4 convolution_bitcast_fusion.5
  120.0 1.6 convolution_bitcast_fusion.4
  121.9 1.9 %convolution_bitcast_fusion.2 = f32[64,32,16]{1,2,0:T(8,128)S(1)} fusion(bf16[64,3,32,32]{3,2,1,0:T(8,128)(2,1)S(1)} %copy-done.3, bf16[64,3,32,16]{2,3,1,0:T(8,128)(2,1)} %bitcast.562, pred[64,3]{1,0:T(8,128)(4,1)S(1)} %copy-done.17), kind=kOutput, calls=%fused_computation.53 | convolution fusion | flops 6389760 | bytes 721088 | tf_op jit(solution)/shard_map/nsab,nsbr->nar/dot_general | solution.py:54
  125.1 7.5 %all-to-all-start.2 = ((bf16[32,2,512]{2,1,0:T(2,128)(2,1)}), bf16[32,2,512]{2,1,0:T(2,128)(2,1)S(1)}, u32[]{:S(2)}, u32[]{:S(2)}) async-start(bf16[32,2,512]{2,1,0:T(2,128)(2,1)} %reshape.484), calls=%async_computation.2 | async-start | bytes 131072 | tf_op jit(solution)/shard_map/all_to_all | solution.py:162
  132.6 8.6 %fusion.3 = f32[16,256,512]{2,1,0:T(8,128)} fusion(bf16[16,256,512]{2,1,0:T(8,128)(2,1)} %bitcast.561, pred[16]{0:T(512)(128)(4,1)S(1)} %copy-done.31, pred[16]{0:T(512)(128)(4,1)S(1)} %copy-done.32, pred[16]{0:T(512)(128)(4,1)S(1)} %copy-done.33, bf16[16,3,256,256]{3,2,1,0:T(8,128)(2,1)} %param.12), kind=kOutput, calls=%fused_computation.14 | convolution fusion | flops 1076887552 | bytes 18874416 | tf_op jit(solution)/shard_map/npq,nqr->npr/dot_general | solution.py:143
  142.7 1.4 fusion.53
  145.2 1.6 fusion.48
  146.9 1.2 convolution_bitcast_fusion
  148.2 6.6 %fusion.46 = f32[16,512,256]{1,2,0:T(8,128)} fusion(bf16[16,256,32]{1,2,0:T(8,128)(2,1)S(1)} %copy-done, f32[16,32,512]{2,1,0:T(8,128)S(1)} %convolution_bitcast_fusion, f32[16,32,512]{2,1,0:T(8,128)S(1)} %fusion.68, f32[16,32,512]{2,1,0:T(8,128)} %fusion.63, f32[16,32,512]{2,1,0:T(8,128)} %fusion.70, bf16[3,32,512]{2,1,0:T(8,128)(2,1)S(1)} %copy-done.7, ...), kind=kOutput, calls=%fused_computation.58 | convolution fusion | flops 152616960 | bytes 13860912 | tf_op jit(solution)/shard_map/npk,nkr->npr/dot_general | solution.py:171
  154.8 15.3 %fusion = bf16[16,256,512]{2,1,0:T(8,128)(2,1)} fusion(f32[16,512,256]{1,2,0:T(8,128)} %fusion.46, f32[16,256,512]{2,1,0:T(8,128)} %fusion.3, f32[16,256,512]{2,1,0:T(8,128)} %fusion.7, bf16[16,256,512]{2,1,0:T(8,128)(2,1)} %bitcast.560, pred[16]{0:T(512)(128)(4,1)S(1)} %copy-done.30, pred[16]{0:T(512)(128)(4,1)S(1)} %copy-done.29, ...), kind=kOutput, calls=%fused_computation.6 | convolution fusion | flops 1085276160 | bytes 39845936 | tf_op jit(solution)/shard_map/npq,nqr->npr/dot_general | solution.py:143
  (195 shorter events, 31.9 us)
Async XLA Ops:
  0.0 148.1 %copy-start = (bf16[16,256,32]{1,2,0:T(8,128)(2,1)S(1)}, bf16[16,256,32]{1,2,0:T(8,128)(2,1)}, u32[]{:S(2)}) copy-start(bf16[16,256,32]{1,2,0:T(8,128)(2,1)} %param.15) | copy-start | bytes 786436
  0.0 6.6 %copy-start.5 = (bf16[28,32,32]{2,1,0:T(8,128)(2,1)S(1)}, bf16[28,32,32]{2,1,0:T(8,128)(2,1)}, u32[]{:S(2)}) copy-start(bf16[28,32,32]{2,1,0:T(8,128)(2,1)} %param.16) | copy-start | bytes 172036
  0.0 26.0 %copy-start.13 = (s32[128,3]{0,1:T(4,128)S(1)}, s32[128,3]{0,1:T(4,128)}, u32[]{:S(2)}) copy-start(s32[128,3]{0,1:T(4,128)} %param.21) | copy-start | bytes 4612
  3.1 27.4 %copy-start.16 = (s32[28,3]{0,1:T(4,128)S(1)}, s32[28,3]{0,1:T(4,128)}, u32[]{:S(2)}) copy-start(s32[28,3]{0,1:T(4,128)} %param.20) | copy-start | bytes 1012
  3.2 28.6 %copy-start.24 = (s32[16,3]{0,1:T(4,128)S(1)}, s32[16,3]{0,1:T(4,128)}, u32[]{:S(2)}) copy-start(s32[16,3]{0,1:T(4,128)} %param.13) | copy-start | bytes 580
  3.2 32.3 %copy-start.14 = (bf16[16,32,32]{2,1,0:T(8,128)(2,1)S(1)}, bf16[16,32,32]{2,1,0:T(8,128)(2,1)}, u32[]{:S(2)}) copy-start(bf16[16,32,32]{2,1,0:T(8,128)(2,1)} %param.17) | copy-start | bytes 98308
  3.2 32.5 %copy-start.12 = (bf16[16,3,32,32]{3,2,1,0:T(8,128)(2,1)S(1)}, bf16[16,3,32,32]{3,2,1,0:T(8,128)(2,1)}, u32[]{:S(2)}) copy-start(bf16[16,3,32,32]{3,2,1,0:T(8,128)(2,1)} %param.19) | copy-start | bytes 294916
  3.2 70.8 %collective-permute-start = (bf16[3,32,512]{2,1,0:T(8,128)(2,1)S(1)}, bf16[3,32,512]{2,1,0:T(8,128)(2,1)S(1)}, u32[]{:S(2)}, u32[]{:S(2)}) collective-permute-start(bf16[3,32,512]{2,1,0:T(8,128)(2,1)S(1)} %get-tuple-element.9), channel_id=1, source_target_pairs={{0,8},{8,16},{16,24},{24,32},{32,40},{40,48},{48,56},{56,64},{64,7... | collective-permute-start | bytes 294920 | tf_op jit(solution)/shard_map/ppermute | solution.py:14
  5.9 53.3 %collective-permute-start.1 = (bf16[3,32,512]{2,1,0:T(8,128)(2,1)S(1)}, bf16[3,32,512]{2,1,0:T(8,128)(2,1)S(1)}, u32[]{:S(2)}, u32[]{:S(2)}) collective-permute-start(bf16[3,32,512]{2,1,0:T(8,128)(2,1)S(1)} %get-tuple-element.10), channel_id=1, source_target_pairs={{8,0},{16,8},{24,16},{32,24},{40,32},{48,40},{56,48},{64,56},{72,6... | collective-permute-start | bytes 294920 | tf_op jit(solution)/shard_map/ppermute | solution.py:16
  7.9 64.3 %collective-permute-start.4 = (bf16[3,32,512]{2,1,0:T(8,128)(2,1)}, bf16[3,32,512]{2,1,0:T(8,128)(2,1)S(1)}, u32[]{:S(2)}, u32[]{:S(2)}) collective-permute-start(bf16[3,32,512]{2,1,0:T(8,128)(2,1)} %get-tuple-element.13), channel_id=1, source_target_pairs={{0,8},{8,16},{16,24},{24,32},{32,40},{40,48},{48,56},{56,64},{64,7... | collective-permute-start | bytes 294920 | tf_op jit(solution)/shard_map/ppermute | solution.py:14
  9.0 57.5 %collective-permute-start.5 = (bf16[3,32,512]{2,1,0:T(8,128)(2,1)}, bf16[3,32,512]{2,1,0:T(8,128)(2,1)S(1)}, u32[]{:S(2)}, u32[]{:S(2)}) collective-permute-start(bf16[3,32,512]{2,1,0:T(8,128)(2,1)} %get-tuple-element.14), channel_id=1, source_target_pairs={{8,0},{16,8},{24,16},{32,24},{40,32},{48,40},{56,48},{64,56},{72,6... | collective-permute-start | bytes 294920 | tf_op jit(solution)/shard_map/ppermute | solution.py:16
  13.5 41.8 %collective-permute-start.3 = (bf16[3,32,512]{2,1,0:T(8,128)(2,1)S(1)}, bf16[3,32,512]{2,1,0:T(8,128)(2,1)S(1)}, u32[]{:S(2)}, u32[]{:S(2)}) collective-permute-start(bf16[3,32,512]{2,1,0:T(8,128)(2,1)S(1)} %get-tuple-element.12), channel_id=1, source_target_pairs={{8,0},{16,8},{24,16},{32,24},{40,32},{48,40},{56,48},{64,56},{72,6... | collective-permute-start | bytes 294920 | tf_op jit(solution)/shard_map/ppermute | solution.py:16
  22.4 23.6 %all-to-all-start.1 = ((bf16[32,2,512]{2,1,0:T(2,128)(2,1)}), bf16[32,2,512]{2,1,0:T(2,128)(2,1)S(1)}, u32[]{:S(2)}, u32[]{:S(2)}) async-start(bf16[32,2,512]{2,1,0:T(2,128)(2,1)} %reshape.482), calls=%async_computation.1 | async-start | bytes 131072 | tf_op jit(solution)/shard_map/all_to_all | solution.py:158
  47.1 35.8 %all-to-all-start = ((bf16[8,16,4096]{2,1,0:T(8,128)(2,1)}), bf16[8,16,4096]{2,1,0:T(8,128)(2,1)}, u32[]{:S(2)}, u32[]{:S(2)}) async-start(bf16[8,16,4096]{2,1,0:T(8,128)(2,1)} %broadcast_in_dim.421), calls=%async_computation | async-start | bytes 2097152 | tf_op jit(solution)/shard_map/all_to_all | solution.py:25
  55.4 8.0 %collective-permute-start.2 = (bf16[3,32,512]{2,1,0:T(8,128)(2,1)}, bf16[3,32,512]{2,1,0:T(8,128)(2,1)S(1)}, u32[]{:S(2)}, u32[]{:S(2)}) collective-permute-start(bf16[3,32,512]{2,1,0:T(8,128)(2,1)} %get-tuple-element.11), channel_id=1, source_target_pairs={{0,8},{8,16},{16,24},{24,32},{32,40},{40,48},{48,56},{56,64},{64,7... | collective-permute-start | bytes 294920 | tf_op jit(solution)/shard_map/ppermute | solution.py:14
  59.2 0.6 copy-start.15
  59.2 17.3 %collective-permute-start.7 = (bf16[256,512]{1,0:T(8,128)(2,1)}, bf16[256,512]{1,0:T(8,128)(2,1)S(1)}, u32[]{:S(2)}, u32[]{:S(2)}) collective-permute-start(bf16[256,512]{1,0:T(8,128)(2,1)} %get-tuple-element.7), channel_id=1, source_target_pairs={{8,0},{16,8},{24,16},{32,24},{40,32},{48,40},{56,48},{64,56},{72,6... | collective-permute-start | bytes 786440 | tf_op jit(solution)/shard_map/ppermute | solution.py:16
  59.8 16.7 %copy-start.1 = (bf16[4096,512]{1,0:T(8,128)(2,1)S(1)}, bf16[4096,512]{1,0:T(8,128)(2,1)}, u32[]{:S(2)}) copy-start(bf16[4096,512]{1,0:T(8,128)(2,1)} %param.11) | copy-start | bytes 12582916
  63.4 16.7 %copy-start.8 = (bf16[3,32,512]{2,1,0:T(8,128)(2,1)}, bf16[3,32,512]{2,1,0:T(8,128)(2,1)S(1)}, u32[]{:S(2)}) copy-start(bf16[3,32,512]{2,1,0:T(8,128)(2,1)S(1)} %collective-permute-done.2) | copy-start | bytes 294916
  63.4 13.1 %collective-permute-start.6 = (bf16[256,512]{1,0:T(8,128)(2,1)}, bf16[256,512]{1,0:T(8,128)(2,1)S(1)}, u32[]{:S(2)}, u32[]{:S(2)}) collective-permute-start(bf16[256,512]{1,0:T(8,128)(2,1)} %get-tuple-element.8), channel_id=1, source_target_pairs={{0,8},{8,16},{16,24},{24,32},{32,40},{40,48},{48,56},{56,64},{64,7... | collective-permute-start | bytes 786440 | tf_op jit(solution)/shard_map/ppermute | solution.py:14
  72.3 7.8 %copy-start.10 = (bf16[3,32,512]{2,1,0:T(8,128)(2,1)}, bf16[3,32,512]{2,1,0:T(8,128)(2,1)S(1)}, u32[]{:S(2)}) copy-start(bf16[3,32,512]{2,1,0:T(8,128)(2,1)S(1)} %collective-permute-done.4) | copy-start | bytes 294916
  74.0 6.1 %copy-start.6 = (bf16[3,32,512]{2,1,0:T(8,128)(2,1)}, bf16[3,32,512]{2,1,0:T(8,128)(2,1)S(1)}, u32[]{:S(2)}) copy-start(bf16[3,32,512]{2,1,0:T(8,128)(2,1)S(1)} %collective-permute-done) | copy-start | bytes 294916
  103.9 16.1 %copy-start.4 = (bf16[96,32,16]{1,2,0:T(8,128)(2,1)S(1)}, bf16[96,32,16]{1,2,0:T(8,128)(2,1)}, u32[]{:S(2)}) copy-start(bf16[96,32,16]{1,2,0:T(8,128)(2,1)} %gather_fusion.1) | copy-start | bytes 294916
  114.8 7.0 %copy-start.3 = (bf16[64,3,32,32]{3,2,1,0:T(8,128)(2,1)S(1)}, bf16[64,3,32,32]{3,2,1,0:T(8,128)(2,1)}, u32[]{:S(2)}) copy-start(bf16[64,3,32,32]{3,2,1,0:T(8,128)(2,1)} %copy.146) | copy-start | bytes 1179652
  114.8 7.0 %copy-start.17 = (pred[64,3]{1,0:T(8,128)(4,1)S(1)}, pred[64,3]{1,0:T(8,128)(4,1)}, u32[]{:S(2)}) copy-start(pred[64,3]{1,0:T(8,128)(4,1)} %copy.142) | copy-start | bytes 580
  119.8 12.8 %copy-start.31 = (pred[16]{0:T(512)(128)(4,1)S(1)}, pred[16]{0:T(512)(128)(4,1)}, u32[]{:S(2)}) copy-start(pred[16]{0:T(512)(128)(4,1)} %get-tuple-element.21) | copy-start | bytes 52
  119.8 12.8 %copy-start.32 = (pred[16]{0:T(512)(128)(4,1)S(1)}, pred[16]{0:T(512)(128)(4,1)}, u32[]{:S(2)}) copy-start(pred[16]{0:T(512)(128)(4,1)} %get-tuple-element.22) | copy-start | bytes 52
  119.8 12.8 %copy-start.33 = (pred[16]{0:T(512)(128)(4,1)S(1)}, pred[16]{0:T(512)(128)(4,1)}, u32[]{:S(2)}) copy-start(pred[16]{0:T(512)(128)(4,1)} %get-tuple-element.23) | copy-start | bytes 52
  125.1 16.2 %all-to-all-start.2 = ((bf16[32,2,512]{2,1,0:T(2,128)(2,1)}), bf16[32,2,512]{2,1,0:T(2,128)(2,1)S(1)}, u32[]{:S(2)}, u32[]{:S(2)}) async-start(bf16[32,2,512]{2,1,0:T(2,128)(2,1)} %reshape.484), calls=%async_computation.2 | async-start | bytes 131072 | tf_op jit(solution)/shard_map/all_to_all | solution.py:162
  132.6 10.1 %copy-start.11 = (bf16[3,32,512]{2,1,0:T(8,128)(2,1)S(1)}, bf16[3,32,512]{2,1,0:T(8,128)(2,1)}, u32[]{:S(2)}) copy-start(bf16[3,32,512]{2,1,0:T(8,128)(2,1)} %copy-done.10) | copy-start | bytes 294916
  132.6 10.1 %copy-start.21 = (pred[4]{0:T(512)(128)(4,1)S(1)}, pred[4]{0:T(512)(128)(4,1)}, u32[]{:S(2)}) copy-start(pred[4]{0:T(512)(128)(4,1)} %get-tuple-element.48) | copy-start | bytes 16
  132.6 10.1 %copy-start.22 = (pred[4]{0:T(512)(128)(4,1)S(1)}, pred[4]{0:T(512)(128)(4,1)}, u32[]{:S(2)}) copy-start(pred[4]{0:T(512)(128)(4,1)} %get-tuple-element.58) | copy-start | bytes 16
  132.6 10.1 %copy-start.23 = (pred[4]{0:T(512)(128)(4,1)S(1)}, pred[4]{0:T(512)(128)(4,1)}, u32[]{:S(2)}) copy-start(pred[4]{0:T(512)(128)(4,1)} %get-tuple-element.59) | copy-start | bytes 16
  141.3 3.9 %copy-start.2 = (f32[8,32,512]{2,1,0:T(8,128)S(1)}, f32[8,32,512]{2,1,0:T(8,128)}, u32[]{:S(2)}) copy-start(f32[8,32,512]{2,1,0:T(8,128)} %fusion.80) | copy-start | bytes 1572868
  141.3 3.9 %copy-start.9 = (bf16[3,32,512]{2,1,0:T(8,128)(2,1)S(1)}, bf16[3,32,512]{2,1,0:T(8,128)(2,1)}, u32[]{:S(2)}) copy-start(bf16[3,32,512]{2,1,0:T(8,128)(2,1)} %copy-done.8) | copy-start | bytes 294916
  141.3 3.9 %copy-start.25 = (pred[8]{0:T(512)(128)(4,1)S(1)}, pred[8]{0:T(512)(128)(4,1)}, u32[]{:S(2)}) copy-start(pred[8]{0:T(512)(128)(4,1)} %get-tuple-element.36) | copy-start | bytes 28
  141.3 4.0 %copy-start.26 = (pred[8]{0:T(512)(128)(4,1)S(1)}, pred[8]{0:T(512)(128)(4,1)}, u32[]{:S(2)}) copy-start(pred[8]{0:T(512)(128)(4,1)} %get-tuple-element.46) | copy-start | bytes 28
  141.3 4.0 %copy-start.27 = (pred[8]{0:T(512)(128)(4,1)S(1)}, pred[8]{0:T(512)(128)(4,1)}, u32[]{:S(2)}) copy-start(pred[8]{0:T(512)(128)(4,1)} %get-tuple-element.47) | copy-start | bytes 28
  141.6 6.5 %copy-start.7 = (bf16[3,32,512]{2,1,0:T(8,128)(2,1)S(1)}, bf16[3,32,512]{2,1,0:T(8,128)(2,1)}, u32[]{:S(2)}) copy-start(bf16[3,32,512]{2,1,0:T(8,128)(2,1)} %copy-done.6) | copy-start | bytes 294916
  141.6 6.5 %copy-start.18 = (pred[16]{0:T(512)(128)(4,1)S(1)}, pred[16]{0:T(512)(128)(4,1)}, u32[]{:S(2)}) copy-start(pred[16]{0:T(512)(128)(4,1)} %get-tuple-element.24) | copy-start | bytes 52
  141.7 6.5 %copy-start.19 = (pred[16]{0:T(512)(128)(4,1)S(1)}, pred[16]{0:T(512)(128)(4,1)}, u32[]{:S(2)}) copy-start(pred[16]{0:T(512)(128)(4,1)} %get-tuple-element.34) | copy-start | bytes 52
  141.7 6.5 %copy-start.20 = (pred[16]{0:T(512)(128)(4,1)S(1)}, pred[16]{0:T(512)(128)(4,1)}, u32[]{:S(2)}) copy-start(pred[16]{0:T(512)(128)(4,1)} %get-tuple-element.35) | copy-start | bytes 52
  148.1 6.6 %copy-start.28 = (pred[16]{0:T(512)(128)(4,1)S(1)}, pred[16]{0:T(512)(128)(4,1)}, u32[]{:S(2)}) copy-start(pred[16]{0:T(512)(128)(4,1)} %get-tuple-element.15) | copy-start | bytes 52
  148.1 6.6 %copy-start.29 = (pred[16]{0:T(512)(128)(4,1)S(1)}, pred[16]{0:T(512)(128)(4,1)}, u32[]{:S(2)}) copy-start(pred[16]{0:T(512)(128)(4,1)} %get-tuple-element.18) | copy-start | bytes 52
  148.2 6.6 %copy-start.30 = (pred[16]{0:T(512)(128)(4,1)S(1)}, pred[16]{0:T(512)(128)(4,1)}, u32[]{:S(2)}) copy-start(pred[16]{0:T(512)(128)(4,1)} %get-tuple-element.20) | copy-start | bytes 52
